TPU v7x, 32 devices: a whole 2x2x4 slice. The times are simulated.
32 devices in a mesh: band: 8 (over z, x), ga: 4 (over y, core).
Axes of the slice: x: 2, y: 2, z: 4, core: 2. Of those that a mesh axis runs over, the one named last changes fastest.
Arguments:
- elements: bfloat16 [2, 768, 2048], P(None, 'band', 'ga'), may hold values from -0.75 to 0.75
- screened: bfloat16 [2, 2, 2048, 2048], P(None, None, 'ga'), may hold values from -0.09375 to 0.09375
- energies: float32 [768], replicated, may hold values from -3 to 3
- freq_points: float32 [2], replicated, may hold values from -3 to 3
- freq_weights: float32 [2], replicated, may hold values from 0.5 to 2
- band_of_slot: int32 [768], replicated, may hold values from 0 to 767, each once
Outputs:
- sigma: float32 [2, 768, 768], P(None, 'band', 'ga')
Inputs may be any that keep to these rules, and one draw needn't show every extreme that they name: `band_of_slot`: each of 0 to 767 stands once.
All inputs are finite; a program needn't handle non-finite values.
Results may differ from a plain program's by a relative error of at most 0.0042.
Values may be sent and summed in bfloat16 or wider, within the bound.
A program may use at most 128 MiB of HBM per device.

v0:
```python
import jax
import jax.numpy as jnp
from jax import lax
from jax.sharding import PartitionSpec as P


def make_left(block):
    flipped = jnp.stack([-block[1], block[0]])
    return jnp.stack([block, flipped])


def on_device(elements, screened, energies, freq_points, freq_weights, band_of_slot):
    bands = elements.shape[1]
    slot_energy = jnp.take(energies, band_of_slot)
    offset = slot_energy[None, :] - freq_points[:, None]
    screen = freq_weights[:, None] / (1.0 + 4.0 * offset * offset)
    own_start = lax.axis_index("band") * bands
    screen_own = lax.dynamic_slice_in_dim(screen, own_start, bands, 1)
    piece = lax.all_gather(elements, "ga", axis=2, tiled=True)
    real_side = jnp.stack([piece[0], -piece[1]])
    imag_side = jnp.stack([piece[1], piece[0]])
    sides = jnp.stack([real_side, imag_side])
    applied = jnp.einsum(
        "dcmk,wcgk->wdmg", sides, screened, preferred_element_type=jnp.float32
    ).astype(jnp.bfloat16)
    left_own = make_left(elements)
    pairs = jnp.einsum(
        "dcnk,wcmk->wdnm",
        left_own,
        lax.all_gather(applied, "band", axis=2, tiled=True),
        preferred_element_type=jnp.float32,
    )
    factor = 0.5 * (screen_own[:, :, None] + screen[:, None, :])
    partial_rows = jnp.sum(pairs * factor[:, None], axis=0)
    return lax.psum_scatter(partial_rows, "ga", scatter_dimension=2, tiled=True)


def solution(mesh):
    placed = (P(None, "band", "ga"), P(None, None, "ga", None), P(), P(), P(), P())
    return jax.shard_map(
        on_device, mesh=mesh, in_specs=placed, out_specs=P(None, "band", "ga"), check_vma=False
    )
```

profile of v0, /device:TPU:0, one launch (start us, length us, event | category | flops | bytes accessed | tf_op | source)
XLA Modules:
  0.0 121.1 jit_solution(2113868990376874802)
XLA Ops:
  6.5 0.0 copy-start
  6.5 0.0 all-gather.2.cloned.1.call-start
  6.5 10.4 %all_gather.6 = bf16[2,96,2048]{2,1,0:T(8,128)(2,1)S(1)} all-gather(bf16[2,96,512]{2,1,0:T(8,128)(2,1)} %param.6), channel_id=1, replica_groups=mesh['band'=8,'ga'=4] {'ga'}, dimensions={2}, use_global_device_ids=true | all-gather | bytes 983040 | tf_op jit(solution)/shard_map/all_gather | solution.py:19
  17.0 0.1 slice_negate_fusion.1
  17.1 0.1 maximum_bitcast_fusion.8
  17.2 0.0 copy-start.2
  17.2 7.0 %fusion.21 = bf16[2,2,96,512]{3,2,1,0:T(8,128)(2,1)} fusion(bf16[2,2,512,2048]{3,2,1,0:T(8,128)(2,1)} %param.7, bf16[1,2,96,2048]{3,2,1,0:T(8,128)(2,1)S(1)} %get-tuple-element.9, bf16[1,2,96,2048]{3,2,1,0:T(8,128)(2,1)S(1)} %get-tuple-element.8), kind=kOutput, calls=%fused_computation.13 | convolution fusion | flops 1613955072 | bytes 10354688 | tf_op jit(solution)/shard_map/dcmk,wcgk->wdmg/dot_general | solution.py:23
  24.2 0.0 copy-start.3
  24.2 0.0 copy-start.4
  24.2 0.0 copy-start.1
  24.2 0.0 all-gather.2.cloned.1.call-update
  24.3 0.0 reduce-scatter.4.cloned.1.call-start
  24.3 0.0 copy-done.2
  24.4 0.0 copy-done
  24.4 3.2 %gather_fusion = f32[768]{0:T(1024)S(1)} fusion(f32[768]{0:T(1024)S(1)} %copy-done, s32[1024]{0:T(1024)S(1)} %pad_clamp_fusion), kind=kCustom, calls=%fused_computation | custom fusion | bytes 9216 | tf_op jit(solution)/shard_map/jit(_take)/gather | solution.py:14
  27.6 0.0 copy-done.3
  27.6 0.0 copy-done.4
  27.6 0.1 fusion.27
  27.7 0.1 constant_dynamic-slice_fusion
  27.8 0.0 copy-done.1
  27.8 0.1 add_multiply_fusion
  27.9 57.3 %all-gather.2.cloned.1.call-done = bf16[2,2,768,512]{3,2,1,0:T(8,128)(2,1)} async-done(((bf16[2,2,96,512]{3,2,1,0:T(8,128)(2,1)}), bf16[2,2,768,512]{3,2,1,0:T(8,128)(2,1)}) %all-gather.2.cloned.1.call-update) | async-done | bytes 3145744 | tf_op jit(solution)/shard_map/all_gather | solution.py:30
  85.3 3.1 %fusion.12 = f32[2,96,768]{2,1,0:T(8,128)S(1)} fusion(bf16[2,2,768,512]{3,2,1,0:T(8,128)(2,1)} %all-gather.2.cloned.1.call-done, f32[2,96,768]{2,1,0:T(8,128)S(1)} %add_multiply_fusion, bf16[1,2,96,512]{3,2,1,0:T(8,128)(2,1)S(1)} %maximum_bitcast_fusion.12, bf16[1,2,96,512]{3,2,1,0:T(8,128)(2,1)S(1)} %bitcast.63), kind=kOutput, calls=%fused_computation.10 | convolution fusion | flops 605208576 | bytes 4718592 | tf_op jit(solution)/shard_map/dcnk,wcmk->wdnm/dot_general | solution.py:27
  88.4 0.5 copy.11
  88.9 1.4 %reshape.63 = f32[768,192]{1,0:T(8,128)} reshape(f32[768,2,96]{2,1,0:T(2,128)S(1)} %bitcast.61) | data formatting | bytes 1179648
  90.2 0.0 reduce-scatter.4.cloned.1.call-update
  90.3 22.0 %reduce-scatter.4.cloned.1.call-done = f32[192,192]{1,0:T(8,128)} async-done(((f32[768,192]{1,0:T(8,128)}), f32[192,192]{1,0:T(8,128)}) %reduce-scatter.4.cloned.1.call-update) | async-done | bytes 147472
  112.3 1.1 reshape.64
  113.4 0.8 copy.12
  (5 shorter events, 0.1 us)
Async XLA Ops:
  6.5 17.8 %copy-start = (f32[768]{0:T(1024)S(1)}, f32[768]{0:T(1024)}, u32[]{:S(2)}) copy-start(f32[768]{0:T(1024)} %param.8) | copy-start | bytes 9220
  6.5 78.7 %all-gather.2.cloned.1.call-start = ((), (), s32[]{:S(2)}) async-start(), calls=%async_computation.1 | async-start | bytes 3538944 | tf_op jit(solution)/shard_map/all_gather | solution.py:30
  17.2 7.1 %copy-start.2 = (s32[768]{0:T(1024)S(1)}, s32[768]{0:T(1024)}, u32[]{:S(2)}) copy-start(s32[768]{0:T(1024)} %param.11) | copy-start | bytes 9220
  24.2 3.3 %copy-start.3 = (f32[2]{0:T(128)S(1)}, f32[2]{0:T(128)}, u32[]{:S(2)}) copy-start(f32[2]{0:T(128)} %param.10) | copy-start | bytes 28
  24.2 3.4 %copy-start.4 = (f32[2]{0:T(128)S(1)}, f32[2]{0:T(128)}, u32[]{:S(2)}) copy-start(f32[2]{0:T(128)} %param.9) | copy-start | bytes 28
  24.2 3.5 %copy-start.1 = (bf16[2,96,512]{2,1,0:T(8,128)(2,1)S(1)}, bf16[2,96,512]{2,1,0:T(8,128)(2,1)}, u32[]{:S(2)}) copy-start(bf16[2,96,512]{2,1,0:T(8,128)(2,1)} %param.6) | copy-start | bytes 589828
  24.3 88.0 %reduce-scatter.4.cloned.1.call-start = ((), (), s32[]{:S(2)}) async-start(), calls=%async_computation.2 | async-start | bytes 983040
Sparse Core Ops, SparseCore 0:
  24.4 60.8 all-gather.1
  90.4 21.8 reduce-scatter.3
where the time goes:
time: 121 us
  waiting for transfers between devices  79.4 us (66%)
  between operations  13.5 us (11%)
  blocking collectives  10.4 us (9%)
  matrix products  10.2 us (8%)
  local copies, waits for them, and re-layouts  7.04 us (6%)
    all_gather x1, waiting for transfers between devices, on_device(): lax.all_gather(applied, 'band', axis=2, tiled=True)  57.3 us
    unnamed x3, waiting for transfers between devices  22.1 us
    all_gather x1, blocking collectives, on_device(): piece = lax.all_gather(elements, 'ga', axis=2, tiled=True)  10.4 us
    dot_general x1, matrix products, on_device(): jnp.einsum('dcmk,wcgk->wdmg', sides, screened, preferred_element_type=jnp...  7.03 us
    unnamed x14, local copies, waits for them, and re-layouts  3.77 us
    gather x1, local copies, waits for them, and re-layouts, on_device(): slot_energy = jnp.take(energies, band_of_slot)  3.19 us
    dot_general x1, matrix products, on_device(): jnp.einsum('dcnk,wcmk->wdnm', left_own, lax.all_gather(applied, 'band', a...  3.12 us
  transfers between devices with their start and end apart: 2, of which 2 were waited for; matrix products, arithmetic and copies ran while one was open for 3% of the time, Pallas kernels for 0%

commit v1 on v0

v1 whole, which is shorter than its diff:
```python
import functools

import jax
import jax.numpy as jnp
from jax import lax
from jax.experimental import pallas as pl
from jax.experimental.pallas import tpu as pltpu
from jax.sharding import PartitionSpec as P

MESH = pl.DeviceIdType.MESH
F32 = jnp.float32
BF16 = jnp.bfloat16
NT = (((1,), (1,)), ((), ()))


def kernel(nb, ng, nx, el, wh, en, bos, fp, fw, out, *scratch):
    (gat, wv, a_ref, e3, scr, held, dsend, drecv, ysend, yrecv, lv, ssend, srecv, own,
     loc_sem, w_sem, up_sem, dn_sem, x_sem, g_recv, d_ss, d_rs, y_ss, y_rs, s_ss, s_rs) = scratch
    rows, depth = el.shape[1], el.shape[2]
    quarter = wh.shape[3] // ng
    nz, ny = nb // nx, ng // 2
    wide = nx * rows
    per = nz // ng
    slots = en.shape[1]
    b, g = lax.axis_index("band"), lax.axis_index("ga")
    z, x = b // nx, lax.rem(b, nx)
    y, c = g // 2, lax.rem(g, 2)
    mate = g + 1 - 2 * c
    xb = z * nx + (nx - 1 - x)

    mine = gat.at[:, pl.ds(pl.multiple_of(b * rows, rows), rows), :]
    local = pltpu.make_async_copy(el, mine, loc_sem)
    local.start()

    def q_of(other, d):
        core = (1 - c) if other else c
        return lax.rem(y + d, ny) * 2 + core

    order = []
    for d in list(range(1, ny)) + [0]:
        order += [(1, d), (0, d)]

    def w_copy(k, w):
        o, d = order[k]
        cols = pl.ds(pl.multiple_of(q_of(o, d) * quarter, quarter), quarter)
        return pltpu.make_async_copy(wh.at[w, :, :, cols], wv.at[w, k], w_sem.at[w, k])

    for k in range(ng):
        for w in range(2):
            w_copy(k, w).start()

    barrier = pltpu.get_barrier_semaphore()

    def greet(band, ga):
        pl.semaphore_signal(barrier, inc=1, device_id=(band, ga), device_id_type=MESH)

    for r in range(1, ng):
        greet(b, lax.rem(g + r, ng))
    greet(xb, g)

    @pl.when(z > 0)
    def _():
        greet(b - nx, g)

    @pl.when(z < nz - 1)
    def _():
        greet(b + nx, g)

    below = jnp.where(z > 0, 1, 0)
    above = jnp.where(z < nz - 1, 1, 0)
    pl.semaphore_wait(barrier, ng + below + above)
    local.wait()

    def block(src):
        return gat.at[:, pl.ds(pl.multiple_of(src * rows, rows), rows), :]

    def send(src, dst, sem):
        ref = block(src)
        return pltpu.make_async_remote_copy(
            src_ref=ref, dst_ref=ref, send_sem=sem, recv_sem=g_recv.at[src],
            device_id=(dst, g), device_id_type=MESH)

    def arrived(src):
        send(src, xb, x_sem.at[0]).wait_recv()

    def fwd_up(s):
        zs = z - s

        @pl.when(zs >= 0)
        def _():
            src = zs * nx + x
            if not (isinstance(s, int) and s == 0):
                arrived(src)

            @pl.when(z < nz - 1)
            def _():
                send(src, b + nx, up_sem.at[zs]).start()

            send(src, xb, x_sem.at[zs]).start()

    def fwd_down(s):
        zs = z + s

        @pl.when(zs < nz)
        def _():
            src = zs * nx + x
            if not (isinstance(s, int) and s == 0):
                arrived(src)

            @pl.when(z > 0)
            def _():
                send(src, b - nx, dn_sem.at[zs]).start()

            if not (isinstance(s, int) and s == 0):
                send(src, xb, x_sem.at[zs]).start()

    def fwd(s):
        fwd_up(s)
        fwd_down(s)

    fwd(0)

    er = gat[0, pl.ds(pl.multiple_of(b * rows, rows), rows), :]
    ei = gat[1, pl.ds(pl.multiple_of(b * rows, rows), rows), :]
    a_ref[:rows, :depth] = er
    a_ref[:rows, depth:] = ei
    a_ref[rows:, :depth] = -ei
    a_ref[rows:, depth:] = er

    def d_copy(d, w):
        return pltpu.make_async_remote_copy(
            src_ref=dsend.at[d, w], dst_ref=drecv.at[d, w], send_sem=d_ss.at[d, w],
            recv_sem=d_rs.at[d, w], device_id=(b, mate), device_id_type=MESH)

    def y_copy(d, w):
        return pltpu.make_async_remote_copy(
            src_ref=ysend.at[d - 1, w], dst_ref=yrecv.at[d - 1, w], send_sem=y_ss.at[d - 1, w],
            recv_sem=y_rs.at[d - 1, w], device_id=(b, lax.rem(y + d, ny) * 2 + c),
            device_id_type=MESH)

    def pass_on(d):
        for w in range(2):
            d_copy(d, w).wait_recv()
            ysend[d - 1, w] = (held[d, w] + drecv[d, w].astype(F32)).astype(BF16)
            y_copy(d, w).start()

    for k in range(ng):
        o, d = order[k]
        for w in range(2):
            w_copy(k, w).wait()
            part = jnp.dot(a_ref[...], wv[w, k].reshape(2 * depth, quarter),
                           preferred_element_type=F32)
            if o:
                dsend[d, w] = part.astype(BF16)
                d_copy(d, w).start()
            else:
                held[d, w] = part
        if o and k >= 2:
            pass_on(order[k - 1][1])

    row = lax.broadcasted_iota(jnp.int32, (16, slots), 0)
    e = en[...]
    hi = e.astype(BF16).astype(F32)
    mid = (e - hi).astype(BF16).astype(F32)
    lo = e - hi - mid
    e3[...] = jnp.where(row == 0, hi, jnp.where(row == 1, mid, jnp.where(row == 2, lo, 0.0))).astype(BF16)
    tile = slots if slots <= 1024 else 8 * rows

    def plane_screen(i, carry):
        slot = bos[i]

        def add(j, acc):
            at = pl.multiple_of(j * tile, tile)
            hit = lax.broadcasted_iota(jnp.int32, (tile, wide), 0) + at == slot
            return acc + jnp.dot(e3[:, pl.ds(at, tile)], jnp.where(hit, 1.0, 0.0).astype(BF16),
                                 preferred_element_type=F32)

        acc = lax.fori_loop(0, slots // tile, add, jnp.zeros((16, wide), F32))
        energy = jnp.sum(acc, axis=0, keepdims=True)
        for w in range(2):
            off = energy - fp[w]
            scr[i, w : w + 1, :] = 0.5 * (fw[w] / (1.0 + 4.0 * off * off))
        return carry

    lax.fori_loop(0, nz, plane_screen, 0)
    pick = lax.broadcasted_iota(jnp.int32, (rows, wide), 1) == (
        lax.broadcasted_iota(jnp.int32, (rows, wide), 0) + x * rows)
    cols = [jnp.sum(jnp.where(pick, scr[z, w : w + 1, :], 0.0), axis=1, keepdims=True)
            for w in range(2)]

    def consume_plane(zs):
        at = pl.ds(pl.multiple_of(zs * wide, wide), wide)
        pr = lax.dot_general(lv[0], gat[0, at, :], NT, preferred_element_type=F32)
        pr = pr + lax.dot_general(lv[1], gat[1, at, :], NT, preferred_element_type=F32)
        f = [cols[w] + scr[zs, w : w + 1, :] for w in range(2)]
        total = [f[0] * pr[i * rows : (i + 1) * rows]
                 + f[1] * pr[(2 + i) * rows : (3 + i) * rows] for i in range(2)]
        q, p = zs // per, lax.rem(zs, per)

        @pl.when(q == g)
        def _():
            for i in range(2):
                own[p, i] = total[i]

        @pl.when(q != g)
        def _():
            for i in range(2):
                ssend[zs, i] = total[i]
            slot = lax.rem(g - q + ng, ng) - 1
            pltpu.make_async_remote_copy(
                src_ref=ssend.at[zs], dst_ref=srecv.at[slot, p], send_sem=s_ss.at[zs],
                recv_sem=s_rs.at[slot, p], device_id=(b, q), device_id_type=MESH).start()

    def consume(s):
        @pl.when(z - s >= 0)
        def _():
            arrived((z - s) * nx + (nx - 1 - x))
            consume_plane(z - s)

        if not (isinstance(s, int) and s == 0):
            @pl.when(z + s < nz)
            def _():
                arrived((z + s) * nx + (nx - 1 - x))
                consume_plane(z + s)

    fwd(1)
    if nz > 2:
        fwd(2)

    for w in range(2):
        total = held[0, w]
        d_copy(0, w).wait_recv()
        total = total + drecv[0, w].astype(F32)
        for d in range(1, ny):
            y_copy(d, w).wait_recv()
            total = total + yrecv[d - 1, w].astype(F32)
        total = total.astype(BF16)
        lv[0, 2 * w * rows : 2 * (w + 1) * rows, :] = total
        lv[1, 2 * w * rows : (2 * w + 1) * rows, :] = -total[rows:]
        lv[1, (2 * w + 1) * rows : (2 * w + 2) * rows, :] = total[:rows]

    consume(0)

    def tail(s, carry):
        consume(s - 2)
        fwd(s)
        return carry

    lax.fori_loop(3, nz, tail, 0)
    for s in range(max(1, nz - 2), nz):
        consume(s)

    def sent(zs, carry):
        src = zs * nx + x

        @pl.when((zs <= z) & (z < nz - 1))
        def _():
            send(src, b + nx, up_sem.at[zs]).wait_send()

        @pl.when((zs >= z) & (z > 0))
        def _():
            send(src, b - nx, dn_sem.at[zs]).wait_send()

        send(src, xb, x_sem.at[zs]).wait_send()

        @pl.when(zs // per != g)
        def _():
            pltpu.make_async_remote_copy(
                src_ref=ssend.at[zs], dst_ref=srecv.at[0, 0], send_sem=s_ss.at[zs],
                recv_sem=s_rs.at[0, 0], device_id=(b, mate), device_id_type=MESH).wait_send()

        return carry

    lax.fori_loop(0, nz, sent, 0)
    for w in range(2):
        for d in range(ny):
            d_copy(d, w).wait_send()
        for d in range(1, ny):
            y_copy(d, w).wait_send()

    def finish(p, carry):
        total = own[p]
        for r in range(ng - 1):
            pltpu.make_async_remote_copy(
                src_ref=ssend.at[0], dst_ref=srecv.at[r, p], send_sem=s_ss.at[0],
                recv_sem=s_rs.at[r, p], device_id=(b, mate), device_id_type=MESH).wait_recv()
            total = total + srecv[r, p]
        out[p] = total
        return carry

    lax.fori_loop(0, per, finish, 0)


def solution(mesh):
    nb, ng = mesh.shape["band"], mesh.shape["ga"]
    nx = 2
    nz = nb // nx
    ny = ng // 2
    per = nz // ng

    def step(elements, screened, energies, freq_points, freq_weights, band_of_slot):
        _, rows, depth = elements.shape
        quarter = screened.shape[3] // ng
        slots = energies.shape[0]
        wide = nx * rows
        any_space = pl.BlockSpec(memory_space=pl.ANY)
        vmem = pl.BlockSpec(memory_space=pltpu.VMEM)
        smem = pl.BlockSpec(memory_space=pltpu.SMEM)
        dma = pltpu.SemaphoreType.DMA
        result = pl.pallas_call(
            functools.partial(kernel, nb, ng, nx),
            out_shape=jax.ShapeDtypeStruct((per, 2, rows, wide), F32),
            in_specs=[any_space, any_space, vmem, vmem, smem, smem],
            out_specs=vmem,
            scratch_shapes=[
                pltpu.VMEM((2, nb * rows, depth), BF16),
                pltpu.VMEM((2, ng, 2, depth, quarter), BF16),
                pltpu.VMEM((2 * rows, 2 * depth), BF16),
                pltpu.VMEM((16, slots), BF16),
                pltpu.VMEM((nz, 2, wide), F32),
                pltpu.VMEM((ny, 2, 2 * rows, quarter), F32),
                pltpu.VMEM((ny, 2, 2 * rows, quarter), BF16),
                pltpu.VMEM((ny, 2, 2 * rows, quarter), BF16),
                pltpu.VMEM((ny - 1, 2, 2 * rows, quarter), BF16),
                pltpu.VMEM((ny - 1, 2, 2 * rows, quarter), BF16),
                pltpu.VMEM((2, 4 * rows, quarter), BF16),
                pltpu.VMEM((nz, 2, rows, wide), F32),
                pltpu.VMEM((ng - 1, per, 2, rows, wide), F32),
                pltpu.VMEM((per, 2, rows, wide), F32),
                dma, dma((2, ng)), dma((nz,)), dma((nz,)), dma((nz,)), dma((nb,)),
                dma((ny, 2)), dma((ny, 2)), dma((ny - 1, 2)), dma((ny - 1, 2)),
                dma((nz,)), dma((ng - 1, per)),
            ],
            compiler_params=pltpu.CompilerParams(
                collective_id=0, has_side_effects=True, vmem_limit_bytes=60 * 1024 * 1024),
        )(elements, screened, energies.reshape(1, slots), band_of_slot.reshape(nz, 1, wide),
          freq_points, freq_weights)
        return jnp.transpose(result, (1, 2, 0, 3)).reshape(2, rows, per * wide)

    placed = (P(None, "band", "ga"), P(None, None, "ga", None), P(), P(), P(), P())
    return jax.shard_map(
        step, mesh=mesh, in_specs=placed, out_specs=P(None, "band", "ga"), check_vma=False
    )
```

time: 121 us -> 37.5 us (0.31)
  waiting for transfers between devices: 79.4 us -> 0 us
  Pallas kernels: 0 us -> 33 us
  between operations: 13.5 us -> 0.01 us
  blocking collectives: 10.4 us -> 0 us
  matrix products: 10.2 us -> 0 us
  local copies, waits for them, and re-layouts: 7.04 us -> 4.24 us
    all_gather x1 -> x0, waiting for transfers between devices: 57.3 us -> none  [on_device(): lax.all_gather(applied, 'band', axis=2, tiled=True)]
    pallas_call x0 -> x1, Pallas kernels: none -> 33 us  [step(): pl.pallas_call(functools.partial(kernel, nb, ng, nx), out_shape=jax.Shape...]
    unnamed x3 -> x0, waiting for transfers between devices: 22.1 us -> none
    all_gather x1 -> x0, blocking collectives: 10.4 us -> none  [on_device(): piece = lax.all_gather(elements, 'ga', axis=2, tiled=True)]
    dot_general x2 -> x0, matrix products: 10.2 us -> none  [the longest x1 7.03 us: on_device(): jnp.einsum('dcmk,wcgk->wdmg', sides, screened, preferred_element_type=jnp...]
    gather x1 -> x0, local copies, waits for them, and re-layouts: 3.19 us -> none  [on_device(): slot_energy = jnp.take(energies, band_of_slot)]
    reshape x0 -> x2, local copies, waits for them, and re-layouts: none -> 2.62 us  [the longest x1 1.36 us: step(): band_of_slot.reshape(nz, 1, wide)]
    unnamed x14 -> x1, local copies, waits for them, and re-layouts: 3.77 us -> 1.62 us
  transfers between devices with their start and end apart: 2 -> 0, of which waited for: 2 -> 0; matrix products, arithmetic and copies ran while one was open for 3% -> 0% of each run, Pallas kernels for 0% -> 0%
where the time goes in v1:
time: 37.5 us; the launch traced here: 37.3 us
  Pallas kernels  33 us (88%)
  local copies, waits for them, and re-layouts  4.24 us (11%)
    pallas_call x1, Pallas kernels, step(): pl.pallas_call(functools.partial(kernel, nb, ng, nx), out_shape=jax.Shape...  33 us
    unnamed x1, local copies, waits for them, and re-layouts  1.62 us
    reshape x1, local copies, waits for them, and re-layouts, step(): band_of_slot.reshape(nz, 1, wide)  1.36 us
    reshape x1, local copies, waits for them, and re-layouts, step(): energies.reshape(1, slots)  1.27 us

profile of v1, /device:TPU:0, one launch (start us, length us, event | category | flops | bytes accessed | tf_op | source)
XLA Modules:
  0.0 37.3 jit_solution(10298307496265730395)
XLA Ops:
  0.0 1.3 %reshape.6.en = f32[1,768]{1,0:T(1,128)} reshape(f32[768]{0:T(1024)} %param.8) | data formatting | bytes 6144 | tf_op jit(solution)/shard_map/reshape | solution.py:336
  1.3 1.4 %reshape.7.bos = s32[4,1,192]{2,1,0:T(1,128)} reshape(s32[768]{0:T(1024)} %param.11) | data formatting | bytes 6144 | tf_op jit(solution)/shard_map/reshape | solution.py:336
  2.6 33.0 %shard_map.64 = f32[1,2,96,192]{3,2,1,0:T(8,128)} custom-call(bf16[2,96,512]{2,1,0:T(8,128)(2,1)} %el.1, bf16[2,2,512,2048]{3,2,1,0:T(8,128)(2,1)} %wh.1, f32[1,768]{1,0:T(1,128)} %reshape.6.en, s32[4,1,192]{2,1,0:T(1,128)} %reshape.7.bos, f32[2]{0:T(128)} %fp.1, f32[2]{0:T(128)} %fw.1), custom_call_target="tpu_custom_call" | custom-call | tf_op jit(solution)/shard_map/pallas_call | solution.py:310
  35.7 1.6 %copy.8 = f32[2,96,192]{2,1,0:T(8,128)} copy(f32[2,96,192]{2,1,0:T(8,128)} %bitcast.1) | data formatting | bytes 294912

commit v2 on v1

v2 whole, which is shorter than its diff:
```python
import functools

import jax
import jax.numpy as jnp
from jax import lax
from jax.experimental import pallas as pl
from jax.experimental.pallas import tpu as pltpu
from jax.sharding import PartitionSpec as P

MESH = pl.DeviceIdType.MESH
F32 = jnp.float32
BF16 = jnp.bfloat16
NT = (((1,), (1,)), ((), ()))


def kernel(nb, ng, nx, el, wh, en, bos, fp, fw, out, *scratch):
    (gat, wv, a_ref, e3, scr, held, dsend, drecv, ysend, yrecv, lv, ssend, srecv, own,
     loc_sem, w_sem, up_sem, dn_sem, x_sem, g_recv, d_ss, d_rs, y_ss, y_rs, s_ss, s_rs) = scratch
    rows, depth = el.shape[1], el.shape[2]
    quarter = wh.shape[3] // ng
    nz, ny = nb // nx, ng // 2
    per = nb // ng
    slots = en.shape[0]
    b, g = lax.axis_index("band"), lax.axis_index("ga")
    z, x = b // nx, lax.rem(b, nx)
    y, c = g // 2, lax.rem(g, 2)
    mate = g + 1 - 2 * c
    xb = z * nx + (nx - 1 - x)

    barrier = pltpu.get_barrier_semaphore()

    def greet(band, ga):
        pl.semaphore_signal(barrier, inc=1, device_id=(band, ga), device_id_type=MESH)

    greet(xb, g)

    @pl.when(z > 0)
    def _():
        greet(b - nx, g)

    @pl.when(z < nz - 1)
    def _():
        greet(b + nx, g)

    for r in range(1, ng):
        greet(b, lax.rem(g + r, ng))

    mine = gat.at[:, pl.ds(pl.multiple_of(b * rows, rows), rows), :]
    local = pltpu.make_async_copy(el, mine, loc_sem)
    local.start()

    def q_of(other, d):
        core = (1 - c) if other else c
        return lax.rem(y + d, ny) * 2 + core

    order = []
    for d in list(range(1, ny)) + [0]:
        order += [(1, d), (0, d)]

    def w_copy(k, w):
        o, d = order[k]
        cols = pl.ds(pl.multiple_of(q_of(o, d) * quarter, quarter), quarter)
        return pltpu.make_async_copy(wh.at[w, :, :, cols], wv.at[w, k], w_sem.at[w, k])

    below = jnp.where(z > 0, 1, 0)
    above = jnp.where(z < nz - 1, 1, 0)
    pl.semaphore_wait(barrier, ng + below + above)
    local.wait()

    def send(src, i, dst, sem):
        ref = gat.at[i, pl.ds(pl.multiple_of(src * rows, rows), rows), :]
        return pltpu.make_async_remote_copy(
            src_ref=ref, dst_ref=ref, send_sem=sem, recv_sem=g_recv.at[src, i],
            device_id=(dst, g), device_id_type=MESH)

    def arrived(src, i):
        send(src, i, xb, x_sem.at[0, i]).wait_recv()

    def fwd_one(s, i, zs, ok, up, down):
        @pl.when(ok)
        def _():
            src = zs * nx + x
            if not (isinstance(s, int) and s == 0):
                arrived(src, i)
            if up:
                @pl.when(z < nz - 1)
                def _():
                    send(src, i, b + nx, up_sem.at[zs, i]).start()

            if down:
                @pl.when(z > 0)
                def _():
                    send(src, i, b - nx, dn_sem.at[zs, i]).start()

            send(src, i, xb, x_sem.at[zs, i]).start()

    def fwd(s):
        for i in range(2):
            if isinstance(s, int) and s == 0:
                fwd_one(0, i, z, z >= 0, True, True)
            else:
                fwd_one(s, i, z - s, z - s >= 0, True, False)
                fwd_one(s, i, z + s, z + s < nz, False, True)

    fwd(0)
    for k in range(ng):
        for w in range(2):
            w_copy(k, w).start()

    row = lax.broadcasted_iota(jnp.int32, (16, slots), 0)
    e = en[...].reshape(1, slots)
    hi = e.astype(BF16).astype(F32)
    mid = (e - hi).astype(BF16).astype(F32)
    lo = e - hi - mid
    e3[...] = jnp.where(row == 0, hi, jnp.where(row == 1, mid, jnp.where(row == 2, lo, 0.0))).astype(BF16)
    tile = slots if slots <= 1024 else 8 * rows

    for u in range(slots // tile):
        slot = bos[u * tile : (u + 1) * tile].reshape(1, tile)

        def add(j, acc):
            at = pl.multiple_of(j * tile, tile)
            hit = lax.broadcasted_iota(jnp.int32, (tile, tile), 0) + at == slot
            return acc + jnp.dot(e3[:, pl.ds(at, tile)], jnp.where(hit, 1.0, 0.0).astype(BF16),
                                 preferred_element_type=F32)

        acc = lax.fori_loop(0, slots // tile, add, jnp.zeros((16, tile), F32))
        energy = jnp.sum(acc, axis=0, keepdims=True)
        for w in range(2):
            off = energy - fp[w]
            value = 0.5 * (fw[w] / (1.0 + 4.0 * off * off))
            for v in range(tile // rows):
                scr[u * (tile // rows) + v, w : w + 1, :] = value[:, v * rows : (v + 1) * rows]
    pick = lax.broadcasted_iota(jnp.int32, (rows, rows), 1) == lax.broadcasted_iota(
        jnp.int32, (rows, rows), 0)
    cols = [jnp.sum(jnp.where(pick, scr[b, w : w + 1, :], 0.0), axis=1, keepdims=True)
            for w in range(2)]

    er = gat[0, pl.ds(pl.multiple_of(b * rows, rows), rows), :]
    ei = gat[1, pl.ds(pl.multiple_of(b * rows, rows), rows), :]
    a_ref[:rows, :depth] = er
    a_ref[:rows, depth:] = ei
    a_ref[rows:, :depth] = -ei
    a_ref[rows:, depth:] = er

    def d_copy(d, w):
        return pltpu.make_async_remote_copy(
            src_ref=dsend.at[d, w], dst_ref=drecv.at[d, w], send_sem=d_ss.at[d, w],
            recv_sem=d_rs.at[d, w], device_id=(b, mate), device_id_type=MESH)

    def y_copy(d, w):
        return pltpu.make_async_remote_copy(
            src_ref=ysend.at[d - 1, w], dst_ref=yrecv.at[d - 1, w], send_sem=y_ss.at[d - 1, w],
            recv_sem=y_rs.at[d - 1, w], device_id=(b, lax.rem(y + d, ny) * 2 + c),
            device_id_type=MESH)

    def pass_on(d):
        for w in range(2):
            d_copy(d, w).wait_recv()
            ysend[d - 1, w] = (held[d, w] + drecv[d, w].astype(F32)).astype(BF16)
            y_copy(d, w).start()

    for k in range(ng):
        o, d = order[k]
        for w in range(2):
            w_copy(k, w).wait()
            part = jnp.dot(a_ref[...], wv[w, k].reshape(2 * depth, quarter),
                           preferred_element_type=F32)
            if o:
                dsend[d, w] = part.astype(BF16)
                d_copy(d, w).start()
            else:
                held[d, w] = part
        if o and k >= 2:
            pass_on(order[k - 1][1])

    def consume_block(k):
        at = pl.ds(pl.multiple_of(k * rows, rows), rows)
        pr = lax.dot_general(lv[0], gat[0, at, :], NT, preferred_element_type=F32)
        pr = pr + lax.dot_general(lv[1], gat[1, at, :], NT, preferred_element_type=F32)
        f = [cols[w] + scr[k, w : w + 1, :] for w in range(2)]
        total = [f[0] * pr[i * rows : (i + 1) * rows]
                 + f[1] * pr[(2 + i) * rows : (3 + i) * rows] for i in range(2)]
        q, p = k // per, lax.rem(k, per)

        @pl.when(q == g)
        def _():
            for i in range(2):
                own[p, i] = total[i]

        @pl.when(q != g)
        def _():
            for i in range(2):
                ssend[k, i] = total[i].astype(BF16)
            slot = lax.rem(g - q + ng, ng) - 1
            pltpu.make_async_remote_copy(
                src_ref=ssend.at[k], dst_ref=srecv.at[slot, p], send_sem=s_ss.at[k],
                recv_sem=s_rs.at[slot, p], device_id=(b, q), device_id_type=MESH).start()

    def each_side(s, act):
        @pl.when(z - s >= 0)
        def _():
            act(z - s)

        if not (isinstance(s, int) and s == 0):
            @pl.when(z + s < nz)
            def _():
                act(z + s)

    def consume_own(s):
        each_side(s, lambda zs: consume_block(zs * nx + x))

    def consume_other(s):
        def act(zs):
            k = zs * nx + (nx - 1 - x)
            for i in range(2):
                arrived(k, i)
            consume_block(k)

        each_side(s, act)

    ahead = min(3, nz - 1)
    for s in range(1, ahead + 1):
        fwd(s)

    for w in range(2):
        total = held[0, w]
        d_copy(0, w).wait_recv()
        total = total + drecv[0, w].astype(F32)
        for d in range(1, ny):
            y_copy(d, w).wait_recv()
            total = total + yrecv[d - 1, w].astype(F32)
        total = total.astype(BF16)
        lv[0, 2 * w * rows : 2 * (w + 1) * rows, :] = total
        lv[1, 2 * w * rows : (2 * w + 1) * rows, :] = -total[rows:]
        lv[1, (2 * w + 1) * rows : (2 * w + 2) * rows, :] = total[:rows]

    for s in range(ahead + 1):
        consume_own(s)

    consume_other(0)

    def tail(s, carry):
        fwd(s)
        consume_own(s)
        consume_other(s - ahead)
        return carry

    lax.fori_loop(ahead + 1, nz, tail, 0)
    for s in range(nz - ahead, nz):
        consume_other(s)

    def sent(zs, carry):
        src = zs * nx + x
        for i in range(2):
            @pl.when((zs <= z) & (z < nz - 1))
            def _():
                send(src, i, b + nx, up_sem.at[zs, i]).wait_send()

            @pl.when((zs >= z) & (z > 0))
            def _():
                send(src, i, b - nx, dn_sem.at[zs, i]).wait_send()

            send(src, i, xb, x_sem.at[zs, i]).wait_send()
        for v in range(nx):
            k = zs * nx + v

            @pl.when(k // per != g)
            def _():
                pltpu.make_async_remote_copy(
                    src_ref=ssend.at[k], dst_ref=srecv.at[0, 0], send_sem=s_ss.at[k],
                    recv_sem=s_rs.at[0, 0], device_id=(b, mate), device_id_type=MESH).wait_send()

        return carry

    lax.fori_loop(0, nz, sent, 0)
    for w in range(2):
        for d in range(ny):
            d_copy(d, w).wait_send()
        for d in range(1, ny):
            y_copy(d, w).wait_send()

    for p in range(per):
        for r in range(ng - 1):
            pltpu.make_async_remote_copy(
                src_ref=ssend.at[0], dst_ref=srecv.at[r, p], send_sem=s_ss.at[0],
                recv_sem=s_rs.at[r, p], device_id=(b, mate), device_id_type=MESH).wait_recv()
        for i in range(2):
            total = own[p, i]
            for r in range(ng - 1):
                total = total + srecv[r, p, i].astype(F32)
            out[i, :, p * rows : (p + 1) * rows] = total


def solution(mesh):
    nb, ng = mesh.shape["band"], mesh.shape["ga"]
    nx = 2
    nz = nb // nx
    ny = ng // 2
    per = nb // ng

    def step(elements, screened, energies, freq_points, freq_weights, band_of_slot):
        _, rows, depth = elements.shape
        quarter = screened.shape[3] // ng
        slots = energies.shape[0]
        any_space = pl.BlockSpec(memory_space=pl.ANY)
        vmem = pl.BlockSpec(memory_space=pltpu.VMEM)
        smem = pl.BlockSpec(memory_space=pltpu.SMEM)
        dma = pltpu.SemaphoreType.DMA
        result = pl.pallas_call(
            functools.partial(kernel, nb, ng, nx),
            out_shape=jax.ShapeDtypeStruct((2, rows, per * rows), F32),
            in_specs=[any_space, any_space, vmem, vmem, smem, smem],
            out_specs=vmem,
            scratch_shapes=[
                pltpu.VMEM((2, nb * rows, depth), BF16),
                pltpu.VMEM((2, ng, 2, depth, quarter), BF16),
                pltpu.VMEM((2 * rows, 2 * depth), BF16),
                pltpu.VMEM((16, slots), BF16),
                pltpu.VMEM((nb, 2, rows), F32),
                pltpu.VMEM((ny, 2, 2 * rows, quarter), F32),
                pltpu.VMEM((ny, 2, 2 * rows, quarter), BF16),
                pltpu.VMEM((ny, 2, 2 * rows, quarter), BF16),
                pltpu.VMEM((ny - 1, 2, 2 * rows, quarter), BF16),
                pltpu.VMEM((ny - 1, 2, 2 * rows, quarter), BF16),
                pltpu.VMEM((2, 4 * rows, quarter), BF16),
                pltpu.VMEM((nb, 2, rows, rows), BF16),
                pltpu.VMEM((ng - 1, per, 2, rows, rows), BF16),
                pltpu.VMEM((per, 2, rows, rows), F32),
                dma, dma((2, ng)), dma((nz, 2)), dma((nz, 2)), dma((nz, 2)), dma((nb, 2)),
                dma((ny, 2)), dma((ny, 2)), dma((ny - 1, 2)), dma((ny - 1, 2)),
                dma((nb,)), dma((ng - 1, per)),
            ],
            compiler_params=pltpu.CompilerParams(
                collective_id=0, has_side_effects=True, vmem_limit_bytes=60 * 1024 * 1024),
        )(elements, screened, energies, band_of_slot, freq_points, freq_weights)
        return result

    placed = (P(None, "band", "ga"), P(None, None, "ga", None), P(), P(), P(), P())
    return jax.shard_map(
        step, mesh=mesh, in_specs=placed, out_specs=P(None, "band", "ga"), check_vma=False
    )
```

time: 37.5 us -> 30.3 us (0.81)
  Pallas kernels: 33 us -> 28.5 us
  local copies, waits for them, and re-layouts: 4.24 us -> 1.62 us
    pallas_call x1, Pallas kernels: 33 us -> 28.5 us  [step(): pl.pallas_call(functools.partial(kernel, nb, ng, nx), out_shape=jax.Shape...]
    reshape x2 -> x0, local copies, waits for them, and re-layouts: 2.62 us -> none  [the longest x1 1.36 us: step(): band_of_slot.reshape(nz, 1, wide)]
where the time goes in v2:
time: 30.3 us; the launch traced here: 30.2 us
  Pallas kernels  28.5 us (94%)
  local copies, waits for them, and re-layouts  1.62 us (5%)
    pallas_call x1, Pallas kernels, step(): pl.pallas_call(functools.partial(kernel, nb, ng, nx), out_shape=jax.Shape...  28.5 us
    unnamed x1, local copies, waits for them, and re-layouts  1.62 us

profile of v2, /device:TPU:0, one launch (start us, length us, event | category | flops | bytes accessed | tf_op | source)
XLA Modules:
  0.0 30.2 jit_solution(11829760145920530265)
XLA Ops:
  0.0 28.5 %shard_map.64 = f32[2,96,192]{2,1,0:T(8,128)} custom-call(bf16[2,96,512]{2,1,0:T(8,128)(2,1)} %el.1, bf16[2,2,512,2048]{3,2,1,0:T(8,128)(2,1)} %wh.1, f32[768]{0:T(1024)} %en.1, s32[768]{0:T(1024)} %bos.1, f32[2]{0:T(128)} %fp.1, f32[2]{0:T(128)} %fw.1), custom_call_target="tpu_custom_call" | custom-call | tf_op jit(solution)/shard_map/pallas_call | solution.py:310
  28.5 1.6 %copy.8 = f32[2,96,192]{2,1,0:T(8,128)} copy(f32[2,96,192]{2,1,0:T(8,128)} %shard_map.64) | data formatting | bytes 294912

commit v3 on v2

--- a/solution.py
+++ b/solution.py
@@ -13,8 +13,8 @@
 NT = (((1,), (1,)), ((), ()))
 
 
-def kernel(nb, ng, nx, el, wh, en, bos, fp, fw, out, *scratch):
-    (gat, wv, a_ref, e3, scr, held, dsend, drecv, ysend, yrecv, lv, ssend, srecv, own,
+def kernel(nb, ng, nx, el, wh, en_h, bos_h, fp_h, fw_h, out, *scratch):
+    (en, bos, fp, fw, in_sem, gat, wv, a_ref, e3, scr, held, dsend, drecv, ysend, yrecv, lv, ssend, srecv, own,
      loc_sem, w_sem, up_sem, dn_sem, x_sem, g_recv, d_ss, d_rs, y_ss, y_rs, s_ss, s_rs) = scratch
     rows, depth = el.shape[1], el.shape[2]
     quarter = wh.shape[3] // ng
@@ -45,9 +45,13 @@
     for r in range(1, ng):
         greet(b, lax.rem(g + r, ng))
 
+    small = [pltpu.make_async_copy(s, t, in_sem.at[i]) for i, (s, t) in enumerate(
+        ((en_h, en), (bos_h, bos), (fp_h, fp), (fw_h, fw)))]
     mine = gat.at[:, pl.ds(pl.multiple_of(b * rows, rows), rows), :]
     local = pltpu.make_async_copy(el, mine, loc_sem)
     local.start()
+    for copy in small:
+        copy.start()
 
     def q_of(other, d):
         core = (1 - c) if other else c
@@ -67,8 +71,13 @@
     pl.semaphore_wait(barrier, ng + below + above)
     local.wait()
 
+    unit = rows // 6
+    pieces = ((0, 2 * unit), (2 * unit, 2 * unit), (4 * unit, unit), (5 * unit, unit))
+    last = len(pieces) - 1
+
     def send(src, i, dst, sem):
-        ref = gat.at[i, pl.ds(pl.multiple_of(src * rows, rows), rows), :]
+        start, size = pieces[i]
+        ref = gat.at[:, pl.ds(pl.multiple_of(src * rows + start, unit), size), :]
         return pltpu.make_async_remote_copy(
             src_ref=ref, dst_ref=ref, send_sem=sem, recv_sem=g_recv.at[src, i],
             device_id=(dst, g), device_id_type=MESH)
@@ -76,37 +85,46 @@
     def arrived(src, i):
         send(src, i, xb, x_sem.at[0, i]).wait_recv()
 
-    def fwd_one(s, i, zs, ok, up, down):
-        @pl.when(ok)
-        def _():
-            src = zs * nx + x
-            if not (isinstance(s, int) and s == 0):
-                arrived(src, i)
-            if up:
-                @pl.when(z < nz - 1)
+    def send_z(src, i, up, down):
+        if up:
+            @pl.when(z < nz - 1)
+            def _():
+                send(src, i, b + nx, up_sem.at[src, i]).start()
+
+        if down:
+            @pl.when(z > 0)
+            def _():
+                send(src, i, b - nx, dn_sem.at[src, i]).start()
+
+    def fwd(s):
+        for i in range(last):
+            for zs, up in ((z - s, True), (z + s, False)):
+                @pl.when((zs >= 0) & (zs < nz))
                 def _():
-                    send(src, i, b + nx, up_sem.at[zs, i]).start()
-
-            if down:
-                @pl.when(z > 0)
-                def _():
-                    send(src, i, b - nx, dn_sem.at[zs, i]).start()
-
-            send(src, i, xb, x_sem.at[zs, i]).start()
-
-    def fwd(s):
-        for i in range(2):
-            if isinstance(s, int) and s == 0:
-                fwd_one(0, i, z, z >= 0, True, True)
-            else:
-                fwd_one(s, i, z - s, z - s >= 0, True, False)
-                fwd_one(s, i, z + s, z + s < nz, False, True)
-
-    fwd(0)
+                    src = zs * nx + x
+                    arrived(src, i)
+                    send_z(src, i, up, not up)
+                    send(src, i, xb, x_sem.at[zs, i]).start()
+
+    def fwd_last(s):
+        for zs, up in ((z - s, True), (z + s, False)):
+            @pl.when((zs >= 0) & (zs < nz))
+            def _():
+                for v in (x, nx - 1 - x):
+                    arrived(zs * nx + v, last)
+                    send_z(zs * nx + v, last, up, not up)
+
+    send(b, last, xb, x_sem.at[z, last]).start()
+    for i in range(last + 1):
+        send_z(b, i, True, True)
+        if i < last:
+            send(b, i, xb, x_sem.at[z, i]).start()
     for k in range(ng):
         for w in range(2):
             w_copy(k, w).start()
 
+    for copy in small:
+        copy.wait()
     row = lax.broadcasted_iota(jnp.int32, (16, slots), 0)
     e = en[...].reshape(1, slots)
     hi = e.astype(BF16).astype(F32)
@@ -213,15 +231,20 @@
     def consume_other(s):
         def act(zs):
             k = zs * nx + (nx - 1 - x)
-            for i in range(2):
+            for i in range(last):
                 arrived(k, i)
             consume_block(k)
 
         each_side(s, act)
 
-    ahead = min(3, nz - 1)
-    for s in range(1, ahead + 1):
-        fwd(s)
+    arrived(xb, last)
+    send_z(xb, last, True, True)
+    ahead = 3
+    fwd(1)
+    fwd(2)
+    fwd_last(1)
+    fwd(3)
+    fwd_last(2)
 
     for w in range(2):
         total = held[0, w]
@@ -235,13 +258,15 @@
         lv[1, 2 * w * rows : (2 * w + 1) * rows, :] = -total[rows:]
         lv[1, (2 * w + 1) * rows : (2 * w + 2) * rows, :] = total[:rows]
 
-    for s in range(ahead + 1):
+    for s in range(ahead):
         consume_own(s)
-
     consume_other(0)
+    fwd_last(ahead)
+    consume_own(ahead)
 
     def tail(s, carry):
         fwd(s)
+        fwd_last(s)
         consume_own(s)
         consume_other(s - ahead)
         return carry
@@ -252,16 +277,25 @@
 
     def sent(zs, carry):
         src = zs * nx + x
-        for i in range(2):
+        def left_z(k, i):
             @pl.when((zs <= z) & (z < nz - 1))
             def _():
-                send(src, i, b + nx, up_sem.at[zs, i]).wait_send()
+                send(k, i, b + nx, up_sem.at[k, i]).wait_send()
 
             @pl.when((zs >= z) & (z > 0))
             def _():
-                send(src, i, b - nx, dn_sem.at[zs, i]).wait_send()
-
+                send(k, i, b - nx, dn_sem.at[k, i]).wait_send()
+
+        for i in range(last + 1):
+            left_z(src, i)
+        left_z(zs * nx + (nx - 1 - x), last)
+        for i in range(last):
             send(src, i, xb, x_sem.at[zs, i]).wait_send()
+
+        @pl.when(zs == z)
+        def _():
+            send(src, last, xb, x_sem.at[zs, last]).wait_send()
+
         for v in range(nx):
             k = zs * nx + v
 
@@ -305,14 +339,15 @@
         slots = energies.shape[0]
         any_space = pl.BlockSpec(memory_space=pl.ANY)
         vmem = pl.BlockSpec(memory_space=pltpu.VMEM)
-        smem = pl.BlockSpec(memory_space=pltpu.SMEM)
         dma = pltpu.SemaphoreType.DMA
         result = pl.pallas_call(
             functools.partial(kernel, nb, ng, nx),
-            out_shape=jax.ShapeDtypeStruct((2, rows, per * rows), F32),
-            in_specs=[any_space, any_space, vmem, vmem, smem, smem],
+            out_shape=pltpu.VMEM((2, rows, per * rows), F32),
+            in_specs=[any_space] * 6,
             out_specs=vmem,
             scratch_shapes=[
+                pltpu.VMEM((slots,), F32), pltpu.VMEM((slots,), jnp.int32),
+                pltpu.SMEM(freq_points.shape, F32), pltpu.SMEM(freq_weights.shape, F32), dma((4,)),
                 pltpu.VMEM((2, nb * rows, depth), BF16),
                 pltpu.VMEM((2, ng, 2, depth, quarter), BF16),
                 pltpu.VMEM((2 * rows, 2 * depth), BF16),
@@ -327,7 +362,7 @@
                 pltpu.VMEM((nb, 2, rows, rows), BF16),
                 pltpu.VMEM((ng - 1, per, 2, rows, rows), BF16),
                 pltpu.VMEM((per, 2, rows, rows), F32),
-                dma, dma((2, ng)), dma((nz, 2)), dma((nz, 2)), dma((nz, 2)), dma((nb, 2)),
+                dma, dma((2, ng)), dma((nb, 4)), dma((nb, 4)), dma((nz, 4)), dma((nb, 4)),
                 dma((ny, 2)), dma((ny, 2)), dma((ny - 1, 2)), dma((ny - 1, 2)),
                 dma((nb,)), dma((ng - 1, per)),
             ],

time: 30.3 us -> 27.7 us (0.914)
  Pallas kernels: 28.5 us -> 26.9 us
  local copies, waits for them, and re-layouts: 1.62 us -> 0.68 us
    pallas_call x1, Pallas kernels: 28.5 us -> 26.9 us  [step(): pl.pallas_call(functools.partial(kernel, nb, ng, nx), out_shape=pltpu.VME...]
    unnamed x1, local copies, waits for them, and re-layouts: 1.62 us -> 0.68 us
where the time goes in v3:
time: 27.7 us; the launch traced here: 27.6 us
  Pallas kernels  26.9 us (97%)
  local copies, waits for them, and re-layouts  0.68 us (2%)
    pallas_call x1, Pallas kernels, step(): pl.pallas_call(functools.partial(kernel, nb, ng, nx), out_shape=pltpu.VME...  26.9 us
    unnamed x1, local copies, waits for them, and re-layouts  0.68 us

profile of v3, /device:TPU:0, one launch (start us, length us, event | category | flops | bytes accessed | tf_op | source)
XLA Modules:
  0.0 27.6 jit_solution(545833757766068500)
XLA Ops:
  0.0 26.9 %shard_map.64 = f32[2,96,192]{2,1,0:T(8,128)S(1)} custom-call(bf16[2,96,512]{2,1,0:T(8,128)(2,1)} %el.1, bf16[2,2,512,2048]{3,2,1,0:T(8,128)(2,1)} %wh.1, f32[768]{0:T(1024)} %en_h.1, s32[768]{0:T(1024)} %bos_h.1, f32[2]{0:T(128)} %fp_h.1, f32[2]{0:T(128)} %fw_h.1), custom_call_target="tpu_custom_call" | custom-call | tf_op jit(solution)/shard_map/pallas_call | solution.py:343
  26.9 0.7 %copy.8 = f32[2,96,192]{2,1,0:T(8,128)} copy(f32[2,96,192]{2,1,0:T(8,128)S(1)} %shard_map.64) | data formatting | bytes 294912

commit v4 on v3

--- a/solution.py
+++ b/solution.py
@@ -68,8 +68,11 @@
 
     below = jnp.where(z > 0, 1, 0)
     above = jnp.where(z < nz - 1, 1, 0)
+    local.wait()
+    for k in range(ng):
+        for w in range(2):
+            w_copy(k, w).start()
     pl.semaphore_wait(barrier, ng + below + above)
-    local.wait()
 
     unit = rows // 6
     pieces = ((0, 2 * unit), (2 * unit, 2 * unit), (4 * unit, unit), (5 * unit, unit))
@@ -96,8 +99,8 @@
             def _():
                 send(src, i, b - nx, dn_sem.at[src, i]).start()
 
-    def fwd(s):
-        for i in range(last):
+    def fwd(s, only=None):
+        for i in range(last) if only is None else (only,):
             for zs, up in ((z - s, True), (z + s, False)):
                 @pl.when((zs >= 0) & (zs < nz))
                 def _():
@@ -119,9 +122,6 @@
         send_z(b, i, True, True)
         if i < last:
             send(b, i, xb, x_sem.at[z, i]).start()
-    for k in range(ng):
-        for w in range(2):
-            w_copy(k, w).start()
 
     for copy in small:
         copy.wait()
@@ -243,8 +243,13 @@
     fwd(1)
     fwd(2)
     fwd_last(1)
-    fwd(3)
-    fwd_last(2)
+    inner = (z > 0) & (z < nz - 1)
+
+    @pl.when(inner)
+    def _():
+        fwd_last(2)
+
+    fwd(ahead, 0)
 
     for w in range(2):
         total = held[0, w]
@@ -258,9 +263,19 @@
         lv[1, 2 * w * rows : (2 * w + 1) * rows, :] = -total[rows:]
         lv[1, (2 * w + 1) * rows : (2 * w + 2) * rows, :] = total[:rows]
 
-    for s in range(ahead):
-        consume_own(s)
+    consume_own(0)
     consume_other(0)
+    consume_own(1)
+    fwd(ahead, 1)
+    consume_other(1)
+    fwd(ahead, 2)
+
+    @pl.when(jnp.logical_not(inner))
+    def _():
+        fwd_last(2)
+
+    consume_own(2)
+    consume_other(2)
     fwd_last(ahead)
     consume_own(ahead)
 
@@ -268,12 +283,11 @@
         fwd(s)
         fwd_last(s)
         consume_own(s)
-        consume_other(s - ahead)
+        consume_other(s - 1)
         return carry
 
     lax.fori_loop(ahead + 1, nz, tail, 0)
-    for s in range(nz - ahead, nz):
-        consume_other(s)
+    consume_other(nz - 1)
 
     def sent(zs, carry):
         src = zs * nx + x

time: 27.7 us -> 27.1 us (0.978)
  Pallas kernels: 26.9 us -> 26.3 us
    pallas_call x1, Pallas kernels: 26.9 us -> 26.3 us  [step(): pl.pallas_call(functools.partial(kernel, nb, ng, nx), out_shape=pltpu.VME...]
where the time goes in v4:
time: 27.1 us; the launch traced here: 27 us
  Pallas kernels  26.3 us (97%)
  local copies, waits for them, and re-layouts  0.68 us (3%)
    pallas_call x1, Pallas kernels, step(): pl.pallas_call(functools.partial(kernel, nb, ng, nx), out_shape=pltpu.VME...  26.3 us
    unnamed x1, local copies, waits for them, and re-layouts  0.68 us

profile of v4, /device:TPU:0, one launch (start us, length us, event | category | flops | bytes accessed | tf_op | source)
XLA Modules:
  0.0 27.0 jit_solution(11146081069808483248)
XLA Ops:
  0.0 26.3 %shard_map.64 = f32[2,96,192]{2,1,0:T(8,128)S(1)} custom-call(bf16[2,96,512]{2,1,0:T(8,128)(2,1)} %el.1, bf16[2,2,512,2048]{3,2,1,0:T(8,128)(2,1)} %wh.1, f32[768]{0:T(1024)} %en_h.1, s32[768]{0:T(1024)} %bos_h.1, f32[2]{0:T(128)} %fp_h.1, f32[2]{0:T(128)} %fw_h.1), custom_call_target="tpu_custom_call" | custom-call | tf_op jit(solution)/shard_map/pallas_call | solution.py:357
  26.3 0.7 %copy.8 = f32[2,96,192]{2,1,0:T(8,128)} copy(f32[2,96,192]{2,1,0:T(8,128)S(1)} %shard_map.64) | data formatting | bytes 294912

commit v5 on v4

--- a/solution.py
+++ b/solution.py
@@ -118,10 +118,9 @@
                     send_z(zs * nx + v, last, up, not up)
 
     send(b, last, xb, x_sem.at[z, last]).start()
-    for i in range(last + 1):
+    for i in range(last):
         send_z(b, i, True, True)
-        if i < last:
-            send(b, i, xb, x_sem.at[z, i]).start()
+        send(b, i, xb, x_sem.at[z, i]).start()
 
     for copy in small:
         copy.wait()
@@ -189,8 +188,8 @@
                 d_copy(d, w).start()
             else:
                 held[d, w] = part
-        if o and k >= 2:
-            pass_on(order[k - 1][1])
+        if d and not o:
+            pass_on(d)
 
     def consume_block(k):
         at = pl.ds(pl.multiple_of(k * rows, rows), rows)
@@ -237,11 +236,12 @@
 
         each_side(s, act)
 
-    arrived(xb, last)
-    send_z(xb, last, True, True)
     ahead = 3
     fwd(1)
     fwd(2)
+    send_z(b, last, True, True)
+    arrived(xb, last)
+    send_z(xb, last, True, True)
     fwd_last(1)
     inner = (z > 0) & (z < nz - 1)
 
@@ -250,6 +250,7 @@
         fwd_last(2)
 
     fwd(ahead, 0)
+    fwd(ahead, 1)
 
     for w in range(2):
         total = held[0, w]
@@ -265,10 +266,9 @@
 
     consume_own(0)
     consume_other(0)
+    fwd(ahead, 2)
     consume_own(1)
-    fwd(ahead, 1)
     consume_other(1)
-    fwd(ahead, 2)
 
     @pl.when(jnp.logical_not(inner))
     def _():

time: 27.1 us -> 28.7 us (1.059)
  Pallas kernels: 26.3 us -> 27.9 us
    pallas_call x1, Pallas kernels: 26.3 us -> 27.9 us  [step(): pl.pallas_call(functools.partial(kernel, nb, ng, nx), out_shape=pltpu.VME...]
where the time goes in v5:
time: 28.7 us; the launch traced here: 28.6 us
  Pallas kernels  27.9 us (97%)
  local copies, waits for them, and re-layouts  0.68 us (2%)
    pallas_call x1, Pallas kernels, step(): pl.pallas_call(functools.partial(kernel, nb, ng, nx), out_shape=pltpu.VME...  27.9 us
    unnamed x1, local copies, waits for them, and re-layouts  0.68 us

profile of v5, /device:TPU:0, one launch (start us, length us, event | category | flops | bytes accessed | tf_op | source)
XLA Modules:
  0.0 28.6 jit_solution(12900516529630113338)
XLA Ops:
  0.0 27.9 %shard_map.64 = f32[2,96,192]{2,1,0:T(8,128)S(1)} custom-call(bf16[2,96,512]{2,1,0:T(8,128)(2,1)} %el.1, bf16[2,2,512,2048]{3,2,1,0:T(8,128)(2,1)} %wh.1, f32[768]{0:T(1024)} %en_h.1, s32[768]{0:T(1024)} %bos_h.1, f32[2]{0:T(128)} %fp_h.1, f32[2]{0:T(128)} %fw_h.1), custom_call_target="tpu_custom_call" | custom-call | tf_op jit(solution)/shard_map/pallas_call | solution.py:357
  27.9 0.7 %copy.8 = f32[2,96,192]{2,1,0:T(8,128)} copy(f32[2,96,192]{2,1,0:T(8,128)S(1)} %shard_map.64) | data formatting | bytes 294912

commit v6 on v5

--- a/solution.py
+++ b/solution.py
@@ -121,6 +121,12 @@
     for i in range(last):
         send_z(b, i, True, True)
         send(b, i, xb, x_sem.at[z, i]).start()
+    inner = (z > 0) & (z < nz - 1)
+    outer = jnp.logical_not(inner)
+
+    @pl.when(outer)
+    def _():
+        send_z(b, last, True, True)
 
     for copy in small:
         copy.wait()
@@ -237,16 +243,20 @@
         each_side(s, act)
 
     ahead = 3
+
+    def mine_last():
+        arrived(xb, last)
+        send_z(xb, last, True, True)
+
+    pl.when(outer)(mine_last)
     fwd(1)
     fwd(2)
-    send_z(b, last, True, True)
-    arrived(xb, last)
-    send_z(xb, last, True, True)
-    fwd_last(1)
-    inner = (z > 0) & (z < nz - 1)
 
     @pl.when(inner)
     def _():
+        send_z(b, last, True, True)
+        mine_last()
+        fwd_last(1)
         fwd_last(2)
 
     fwd(ahead, 0)
@@ -267,13 +277,10 @@
     consume_own(0)
     consume_other(0)
     fwd(ahead, 2)
+    pl.when(outer)(lambda: fwd_last(1))
     consume_own(1)
     consume_other(1)
-
-    @pl.when(jnp.logical_not(inner))
-    def _():
-        fwd_last(2)
-
+    pl.when(outer)(lambda: fwd_last(2))
     consume_own(2)
     consume_other(2)
     fwd_last(ahead)

time: 28.7 us -> 28.4 us (0.990)
  Pallas kernels: 27.9 us -> 27.6 us
where the time goes in v6:
time: 28.4 us; the launch traced here: 28.3 us
  Pallas kernels  27.6 us (97%)
  local copies, waits for them, and re-layouts  0.68 us (2%)
    pallas_call x1, Pallas kernels, step(): pl.pallas_call(functools.partial(kernel, nb, ng, nx), out_shape=pltpu.VME...  27.6 us
    unnamed x1, local copies, waits for them, and re-layouts  0.68 us

profile of v6, /device:TPU:0, one launch (start us, length us, event | category | flops | bytes accessed | tf_op | source)
XLA Modules:
  0.0 28.3 jit_solution(6109637589501125489)
XLA Ops:
  0.0 27.6 %shard_map.64 = f32[2,96,192]{2,1,0:T(8,128)S(1)} custom-call(bf16[2,96,512]{2,1,0:T(8,128)(2,1)} %el.1, bf16[2,2,512,2048]{3,2,1,0:T(8,128)(2,1)} %wh.1, f32[768]{0:T(1024)} %en_h.1, s32[768]{0:T(1024)} %bos_h.1, f32[2]{0:T(128)} %fp_h.1, f32[2]{0:T(128)} %fw_h.1), custom_call_target="tpu_custom_call" | custom-call | tf_op jit(solution)/shard_map/pallas_call | solution.py:364
  27.6 0.7 %copy.8 = f32[2,96,192]{2,1,0:T(8,128)} copy(f32[2,96,192]{2,1,0:T(8,128)S(1)} %shard_map.64) | data formatting | bytes 294912
